TPU v7x, 128 devices: a whole 4x4x4 slice. The times are simulated.
128 devices in a mesh: edp: 2 (over z_lo), ep: 64 (over z_hi, x, y, core).
Axes of the slice: x: 4, y: 4, z: 4 (z_hi: 2, z_lo: 2; z = z_hi * 2 + z_lo), core: 2. Of those that a mesh axis runs over, the one named last changes fastest.
Arguments:
- tokens: bfloat16 [16384, 3584], P(('edp', 'ep')), may hold values from -6 to 6
- node_ids: int32 [16384, 4], P(('edp', 'ep')), may hold values from 0 to 7, as said below
- local_ids: int32 [16384, 8], P(('edp', 'ep')), may hold values from 0 to 15, as said below
- affinity: float32 [16384, 8], P(('edp', 'ep')), may hold values from 0.2 to 1
- w_gate: bfloat16 [128, 3584, 1024], P(('edp', 'ep')), may hold values from -0.09375 to 0.09375
- w_up: bfloat16 [128, 3584, 1024], P(('edp', 'ep')), may hold values from -0.09375 to 0.09375
- w_down: bfloat16 [128, 1024, 3584], P(('edp', 'ep')), may hold values from -0.1875 to 0.1875
- grad_parts: float32 [128, 3584, 128], P(('edp', 'ep')), may hold values from -2.5 to 2.5
Outputs:
- mixed: bfloat16 [16384, 3584], P(('edp', 'ep'))
- router_grad: float32 [3584, 128], P(('edp', 'ep'))
Inputs may be any that keep to these rules, and one draw needn't show every extreme that they name: `node_ids`: A token's 4 nodes are distinct and increasing. `local_ids`: columns 2 j and 2 j + 1 name the two experts 2 m and 2 m + 1 of one pair m of node node_ids[t, j], in either order. From the 128 tokens of one device each expert receives at most 10 routes; inside a node the loads from one device differ by at most one.
All inputs are finite; a program needn't handle non-finite values.
Results may differ from a plain program's by a relative error of at most 0.0057.
Values may be sent and summed in bfloat16 or wider, within the bound.
No kernel may reach another device: no remote copies, remote signals or barrier semaphores. Data moves between devices by JAX's collectives and lax.ppermute only.
A program may use at most 192 MiB of HBM per device.

v0:
```python
import jax
import jax.numpy as jnp
from jax import lax
from jax.sharding import PartitionSpec as P

GROUPS = 8


def from_partner(block, axis, bit):
    count = lax.axis_size(axis)
    route = []
    for low in range(count):
        high = low | 1 << bit
        if high != low and high < count:
            route += [(low, high), (high, low)]
    return lax.ppermute(block, axis, route)


def split_up(array, dim, count):
    before, after = (array.shape[:dim], array.shape[dim + 1 :])
    return jnp.moveaxis(array.reshape(*before, count, -1, *after), dim, 0)


def sent_and_summed(array, axis, dim):
    parts = split_up(array, dim, lax.axis_size(axis))
    arrived = lax.all_to_all(parts, axis, split_axis=0, concat_axis=0, tiled=True)
    return arrived.astype(jnp.float32).sum(axis=0)


def sum_at_owner(array, axis, dim):
    parts = split_up(array, dim, lax.axis_size(axis))
    arrived = lax.all_to_all(parts, axis, split_axis=0, concat_axis=0, tiled=True)
    return arrived.sum(axis=0)


def body(tokens, node_ids, local_ids, affinity, w_gate, w_up, w_down, grad_parts):
    edp_count = lax.axis_size("edp")
    ep_count = lax.axis_size("ep")
    experts = edp_count * ep_count
    tok_rows, model_width = tokens.shape
    top_routes = local_ids.shape[1]
    node_pick = node_ids.shape[1]
    capacity = 10 * tok_rows // experts
    per_node = experts // GROUPS
    expert = jnp.repeat(node_ids, top_routes // node_pick, axis=1) * per_node + local_ids
    weight = 2.5 * affinity / jnp.sum(affinity, axis=1, keepdims=True)
    pair_total = experts // 2
    half_cap = (capacity + 1) // 2
    lead_expert = expert[:, 0::2]
    flat_pair = (lead_expert // 2).reshape(-1)
    pair_hot = (flat_pair[:, None] == jnp.arange(pair_total, dtype=jnp.int32)[None, :]).astype(
        jnp.int32
    )
    pair_before = jnp.cumsum(pair_hot, axis=0) - pair_hot
    pair_rank = jnp.sum(pair_before * pair_hot, axis=1)
    dest_device = 2 * flat_pair + pair_rank % 2
    pair_target = dest_device * half_cap + pair_rank // 2
    node_rows = jnp.arange(tok_rows * node_pick, dtype=jnp.int32)
    pair_owner = jnp.zeros((experts * half_cap,), jnp.int32).at[pair_target].set(node_rows + 1)
    pair_filled = pair_owner > 0
    pair_picked = tokens[jnp.maximum(pair_owner - 1, 0) // node_pick]
    pair_send = jnp.where(pair_filled[:, None], pair_picked, jnp.zeros((), jnp.bfloat16))
    pair_send = pair_send.reshape(experts, half_cap, model_width)
    own_rows = lax.all_to_all(pair_send, ("edp", "ep"), split_axis=0, concat_axis=0, tiled=True)
    partner_rows = from_partner(own_rows, "ep", 0)
    received = jnp.concatenate([own_rows, partner_rows], axis=1)
    in_shape = received.shape
    row_block = received.reshape(-1, model_width)
    gate_act = jnp.dot(row_block, w_gate[0], preferred_element_type=jnp.float32)
    up_act = jnp.dot(row_block, w_up[0], preferred_element_type=jnp.float32)
    hidden = (jax.nn.silu(gate_act) * up_act).astype(jnp.bfloat16)
    result = jnp.dot(hidden, w_down[0], preferred_element_type=jnp.float32).astype(jnp.bfloat16)
    both_out = result.reshape(in_shape)
    own_out = both_out[:, :half_cap]
    partner_out = from_partner(both_out[:, half_cap:], "ep", 0)
    back_own, back_partner = (
        lax.all_to_all(own_out, ("edp", "ep"), split_axis=0, concat_axis=0, tiled=True),
        lax.all_to_all(partner_out, ("edp", "ep"), split_axis=0, concat_axis=0, tiled=True),
    )
    back_own = back_own.reshape(experts * half_cap, model_width)[pair_target]
    back_partner = back_partner.reshape(experts * half_cap, model_width)[pair_target]
    back_own = back_own.reshape(tok_rows, node_pick, model_width)
    back_partner = back_partner.reshape(tok_rows, node_pick, model_width)
    is_own = (lead_expert == dest_device.reshape(tok_rows, node_pick))[:, :, None]
    even_out = jnp.where(is_own, back_own, back_partner)
    odd_out = jnp.where(is_own, back_partner, back_own)
    mixed_sum = jnp.zeros((tok_rows, model_width), jnp.float32)
    for column in range(node_pick):
        mixed_sum = mixed_sum + weight[:, 2 * column : 2 * column + 1] * even_out[
            :, column, :
        ].astype(jnp.float32)
        mixed_sum = mixed_sum + weight[:, 2 * column + 1 : 2 * column + 2] * odd_out[
            :, column, :
        ].astype(jnp.float32)
    half_sum = sent_and_summed(grad_parts[0].astype(jnp.bfloat16), "edp", 0)
    router_grad = sum_at_owner(half_sum, "ep", 0)
    return (mixed_sum.astype(jnp.bfloat16), router_grad)


def solution(mesh):
    placed = (
        P(("edp", "ep"), None),
        P(("edp", "ep"), None),
        P(("edp", "ep"), None),
        P(("edp", "ep"), None),
        P(("edp", "ep"), None, None),
        P(("edp", "ep"), None, None),
        P(("edp", "ep"), None, None),
        P(("edp", "ep"), None, None),
    )
    return jax.shard_map(
        body,
        mesh=mesh,
        in_specs=placed,
        out_specs=(P(("edp", "ep"), None), P(("edp", "ep"), None)),
        check_vma=False,
    )
```

profile of v0, /device:TPU:10, one launch (start us, length us, event | category | flops | bytes accessed | tf_op | source)
XLA Modules:
  0.0 513.6 jit_solution(1876373283971529542)
XLA Ops:
  0.6 0.0 copy-start
  0.6 0.8 broadcast_multiply_fusion.1
  1.4 0.7 add.100
  2.1 0.1 copy.48
  2.3 0.1 eq.30
  2.4 0.1 eq.34
  2.5 1.2 reduce-window.6
  3.7 0.2 slice_reduce_fusion
  4.0 0.1 copy.54
  4.1 0.1 mul.148
  4.2 0.1 fusion.16
  4.4 2.4 scatter_custom_fusion
  6.9 0.0 copy-done
  6.9 5.2 %gather_fusion = bf16[640,3584]{1,0:T(8,128)(2,1)} fusion(bf16[128,3584]{1,0:T(8,128)(2,1)S(1)} %copy-done, s32[1024]{0:T(1024)S(1)} %pad_clamp_fusion.1), kind=kCustom, calls=%fused_computation | custom fusion | bytes 9177600 | tf_op jit(solution)/shard_map/gather | solution.py:61
  12.1 7.9 %gather.12 = bf16[128,5,3584]{2,1,0:T(8,128)(2,1)} reshape(bf16[640,3584]{1,0:T(8,128)(2,1)} %gather_fusion) | data formatting | bytes 9175040 | tf_op jit(solution)/shard_map/gather | solution.py:61
  19.9 0.2 broadcast_in_dim.40
  20.1 3.8 broadcast_select_fusion
  24.0 99.0 %all_to_all.25 = bf16[128,5,3584]{2,1,0:T(8,128)(2,1)S(1)} all-to-all(bf16[128,5,3584]{2,1,0:T(8,128)(2,1)S(1)} %broadcast_select_fusion), channel_id=1, replica_groups=mesh['edp'=2,'ep'=64] {'edp','ep'}, dimensions={0} | all-to-all | bytes 9175040 | tf_op jit(solution)/shard_map/all_to_all | solution.py:64
  123.0 0.0 copy-start.2
  123.0 0.0 copy-start.4
  123.0 3.6 copy.55
  126.6 0.8 copy-done.2
  127.4 0.3 collective-permute-start
  127.8 0.0 copy-done.4
  127.8 0.1 convert_element_type.95
  127.9 15.2 %all_to_all.26 = bf16[2,1792,128]{2,1,0:T(8,128)(2,1)S(1)} all-to-all(bf16[2,1792,128]{2,1,0:T(8,128)(2,1)S(1)} %bitcast.90), channel_id=1, replica_groups=mesh['edp'=2,'ep'=64] {'edp'}, dimensions={0} | all-to-all | bytes 1835008 | tf_op jit(solution)/shard_map/all_to_all | solution.py:26
  143.1 0.1 convert_reduce_fusion
  143.3 1.0 reshape.182
  144.3 12.8 %all-to-all-start.4 = ((f32[64,28,128]{2,1,0:T(8,128)}), f32[64,28,128]{2,1,0:T(8,128)S(1)}, u32[]{:S(2)}, u32[]{:S(2)}) async-start(f32[64,28,128]{2,1,0:T(8,128)} %reshape.182), calls=%async_computation.4 | async-start | bytes 2097152 | tf_op jit(solution)/shard_map/all_to_all | solution.py:32
  157.1 0.0 collective-permute-done
  157.1 4.9 copy.56
  162.0 11.9 %pad_maximum_fusion = bf16[128,10,3584]{2,1,0:T(8,128)(2,1)} fusion(bf16[128,5,3584]{2,1,0:T(8,128)(2,1)S(1)} %copy.56, bf16[128,5,3584]{2,1,0:T(8,128)(2,1)} %copy-done.2), kind=kLoop, calls=%fused_computation.5 | loop fusion | flops 18350080 | bytes 18350080 | tf_op jit(solution)/shard_map/concatenate | solution.py:66
  173.9 14.6 %reshape.176 = bf16[1280,3584]{1,0:T(8,128)(2,1)} reshape(bf16[128,10,3584]{2,1,0:T(8,128)(2,1)} %pad_maximum_fusion) | data formatting | bytes 18350080 | tf_op jit(solution)/shard_map/reshape | solution.py:68
  188.5 13.7 %fusion.1 = f32[1280,1024]{1,0:T(8,128)S(1)} fusion(bf16[1280,3584]{1,0:T(8,128)(2,1)} %reshape.176, bf16[1,3584,1024]{2,1,0:T(8,128)(2,1)} %param.13), kind=kOutput, calls=%fused_computation.7 | convolution fusion | flops 9395240960 | bytes 21757952 | tf_op jit(solution)/shard_map/dot_general | solution.py:70
  202.2 0.0 copy-done.3
  202.2 0.0 slice-start.1
  202.2 13.6 %fusion.3 = f32[1280,1024]{1,0:T(8,128)} fusion(bf16[1280,3584]{1,0:T(8,128)(2,1)S(1)} %copy-done.3, bf16[1,3584,1024]{2,1,0:T(8,128)(2,1)} %param.12), kind=kOutput, calls=%fused_computation.9 | convolution fusion | flops 9395240960 | bytes 21757952 | tf_op jit(solution)/shard_map/dot_general | solution.py:69
  215.8 0.0 slice-done
  215.8 0.0 slice-done.1
  215.8 16.3 %convolution_convert_fusion = bf16[1280,3584]{1,0:T(8,128)(2,1)} fusion(bf16[1,1024,3584]{2,1,0:T(8,128)(2,1)S(1)} %bitcast.96, f32[1280,1024]{1,0:T(8,128)S(1)} %fusion.1, f32[1280,1024]{1,0:T(8,128)} %fusion.3), kind=kOutput, calls=%fused_computation.4 | convolution fusion | flops 9407692800 | bytes 27000832 | tf_op jit(solution)/shard_map/dot_general | solution.py:72
  232.2 14.2 %reshape.177 = bf16[128,10,3584]{2,1,0:T(8,128)(2,1)} reshape(bf16[1280,3584]{1,0:T(8,128)(2,1)} %convolution_convert_fusion) | data formatting | bytes 18350080 | tf_op jit(solution)/shard_map/reshape | solution.py:73
  246.4 10.5 %fusion.28 = (bf16[128,5,3584]{2,1,0:T(8,128)(2,1)}, bf16[128,5,3584]{2,1,0:T(8,128)(2,1)S(1)}) fusion(bf16[128,10,3584]{2,1,0:T(8,128)(2,1)} %reshape.177), kind=kLoop, calls=%fused_computation.94 | loop fusion | bytes 18350080 | tf_op jit(solution)/shard_map/slice | solution.py:74
  256.9 3.6 copy.57
  260.5 0.1 collective-permute-start.1
  260.7 0.0 all-to-all-done.4
  260.7 9.8 %all-to-all-start.1 = ((bf16[128,5,3584]{2,1,0:T(8,128)(2,1)}), bf16[128,5,3584]{2,1,0:T(8,128)(2,1)}, u32[]{:S(2)}, u32[]{:S(2)}) async-start(bf16[128,5,3584]{2,1,0:T(8,128)(2,1)} %get-tuple-element.4), calls=%async_computation.1 | async-start | bytes 14680064 | tf_op jit(solution)/shard_map/all_to_all | solution.py:77
  270.5 0.0 collective-permute-done.1
  270.5 7.9 %copy.58 = bf16[128,5,3584]{2,1,0:T(8,128)(2,1)} copy(bf16[128,5,3584]{2,0,1:T(8,128)(2,1)} %collective-permute-done.1) | data formatting | bytes 9175040 | tf_op jit(solution)/shard_map/ppermute | solution.py:16
  278.4 92.3 %all-to-all-done.1 = bf16[128,5,3584]{2,1,0:T(8,128)(2,1)} async-done(((bf16[128,5,3584]{2,1,0:T(8,128)(2,1)}), bf16[128,5,3584]{2,1,0:T(8,128)(2,1)}, u32[]{:S(2)}, u32[]{:S(2)}) %all-to-all-start.1) | async-done | bytes 4587552 | tf_op jit(solution)/shard_map/all_to_all | solution.py:77
  370.7 5.2 %all-to-all-start.2 = ((bf16[128,5,3584]{2,1,0:T(8,128)(2,1)}), bf16[128,5,3584]{2,1,0:T(8,128)(2,1)}, u32[]{:S(2)}, u32[]{:S(2)}) async-start(bf16[128,5,3584]{2,1,0:T(8,128)(2,1)} %copy.58), calls=%async_computation.2 | async-start | bytes 14680064 | tf_op jit(solution)/shard_map/all_to_all | solution.py:78
  375.9 0.1 reduce_sum.42
  376.0 0.1 copy.51
  376.1 0.0 copy-done.5
  376.2 0.7 reduce_sum.45
  376.9 8.1 %reshape.178 = bf16[640,3584]{1,0:T(8,128)(2,1)} reshape(bf16[128,5,3584]{2,1,0:T(8,128)(2,1)} %all-to-all-done.1) | data formatting | bytes 9175040 | tf_op jit(solution)/shard_map/reshape | solution.py:80
  384.9 10.8 %gather_fusion.1 = bf16[512,3584]{1,0:T(8,128)(2,1)} fusion(bf16[640,3584]{1,0:T(8,128)(2,1)} %reshape.178, s32[1024]{0:T(1024)S(1)} %pad_clamp_fusion), kind=kCustom, calls=%fused_computation.1 | custom fusion | bytes 7342080 | tf_op jit(solution)/shard_map/gather | solution.py:80
  395.7 7.0 %reshape.179 = bf16[128,4,3584]{2,1,0:T(4,128)(2,1)} reshape(bf16[512,3584]{1,0:T(8,128)(2,1)} %gather_fusion.1) | data formatting | bytes 7340032 | tf_op jit(solution)/shard_map/reshape | solution.py:82
  402.8 74.3 %all-to-all-done.2 = bf16[128,5,3584]{2,1,0:T(8,128)(2,1)} async-done(((bf16[128,5,3584]{2,1,0:T(8,128)(2,1)}), bf16[128,5,3584]{2,1,0:T(8,128)(2,1)}, u32[]{:S(2)}, u32[]{:S(2)}) %all-to-all-start.2) | async-done | bytes 4587552 | tf_op jit(solution)/shard_map/all_to_all | solution.py:78
  477.1 8.1 %reshape.180 = bf16[640,3584]{1,0:T(8,128)(2,1)} reshape(bf16[128,5,3584]{2,1,0:T(8,128)(2,1)} %all-to-all-done.2) | data formatting | bytes 9175040 | tf_op jit(solution)/shard_map/reshape | solution.py:81
  485.2 10.8 %gather_fusion.2 = bf16[512,3584]{1,0:T(8,128)(2,1)} fusion(bf16[640,3584]{1,0:T(8,128)(2,1)} %reshape.180, s32[1024]{0:T(1024)S(1)} %pad_clamp_fusion), kind=kCustom, calls=%fused_computation.2 | custom fusion | bytes 7342080 | tf_op jit(solution)/shard_map/gather | solution.py:81
  496.0 7.0 %reshape.181 = bf16[128,4,3584]{2,1,0:T(4,128)(2,1)} reshape(bf16[512,3584]{1,0:T(8,128)(2,1)} %gather_fusion.2) | data formatting | bytes 7340032 | tf_op jit(solution)/shard_map/reshape | solution.py:83
  503.0 7.6 %broadcast_select_fusion.2 = (bf16[128,4,3584]{2,0,1:T(8,128)(2,1)S(1)}, bf16[128,4,3584]{2,0,1:T(8,128)(2,1)S(1)}) fusion(pred[128,4]{0,1:T(4,128)(4,1)S(1)} %fusion.23, bf16[128,4,3584]{2,1,0:T(4,128)(2,1)} %reshape.181, bf16[128,4,3584]{2,1,0:T(4,128)(2,1)} %reshape.179), kind=kLoop, calls=%fused_computation.14 | loop fusion | flops 3670016 | bytes 14680576 | tf_op jit(solution)/shard_map/jit(_where)/select_n | solution.py:85
  510.6 2.5 fusion.7
  513.1 0.0 copy-done.1
  (21 shorter events, 0.2 us)
Async XLA Ops:
  0.6 6.2 %copy-start = (bf16[128,3584]{1,0:T(8,128)(2,1)S(1)}, bf16[128,3584]{1,0:T(8,128)(2,1)}, u32[]{:S(2)}) copy-start(bf16[128,3584]{1,0:T(8,128)(2,1)} %param.8) | copy-start | bytes 2752516
  123.0 4.5 copy-start.2
  123.0 4.8 copy-start.4
  127.4 29.7 %collective-permute-start = (bf16[128,5,3584]{2,0,1:T(8,128)(2,1)}, bf16[128,5,3584]{2,0,1:T(8,128)(2,1)}, u32[]{:S(2)}, u32[]{:S(2)}) collective-permute-start(bf16[128,5,3584]{2,0,1:T(8,128)(2,1)} %copy.55), channel_id=1, source_target_pairs={{0,1},{1,0},{2,3},{3,2},{4,5},{5,4},{6,7},{7,6},{8,9},{9,8},{10,11... | collective-permute-start | bytes 13762568 | tf_op jit(solution)/shard_map/ppermute | solution.py:16
  144.3 116.4 %all-to-all-start.4 = ((f32[64,28,128]{2,1,0:T(8,128)}), f32[64,28,128]{2,1,0:T(8,128)S(1)}, u32[]{:S(2)}, u32[]{:S(2)}) async-start(f32[64,28,128]{2,1,0:T(8,128)} %reshape.182), calls=%async_computation.4 | async-start | bytes 2097152 | tf_op jit(solution)/shard_map/all_to_all | solution.py:32
  188.5 13.7 %copy-start.3 = (bf16[1280,3584]{1,0:T(8,128)(2,1)S(1)}, bf16[1280,3584]{1,0:T(8,128)(2,1)}, u32[]{:S(2)}) copy-start(bf16[1280,3584]{1,0:T(8,128)(2,1)} %reshape.176) | copy-start | bytes 27525124
  188.5 27.3 %slice-start = ((s8[7340032]{0:T(1024)(128)(4,1)}), s8[4194304]{0:T(1024)(128)(4,1)S(1)}, s32[]{:S(2)}) async-start(s8[7340032]{0:T(1024)(128)(4,1)} %bitcast.95), calls=%async_computation.5 | async-start | bytes 8388608
  202.2 13.6 %slice-start.1 = ((s8[7340032]{0:T(1024)(128)(4,1)}), s8[3145728]{0:T(1024)(128)(4,1)S(1)}, s32[]{:S(2)}) async-start(s8[7340032]{0:T(1024)(128)(4,1)} %bitcast.95), calls=%async_computation.6 | async-start | bytes 6291456
  260.5 10.0 %collective-permute-start.1 = (bf16[128,5,3584]{2,0,1:T(8,128)(2,1)}, bf16[128,5,3584]{2,0,1:T(8,128)(2,1)}, u32[]{:S(2)}, u32[]{:S(2)}) collective-permute-start(bf16[128,5,3584]{2,0,1:T(8,128)(2,1)} %copy.57), channel_id=1, source_target_pairs={{0,1},{1,0},{2,3},{3,2},{4,5},{5,4},{6,7},{7,6},{8,9},{9,8},{10,11... | collective-permute-start | bytes 13762568 | tf_op jit(solution)/shard_map/ppermute | solution.py:16
  260.7 110.1 %all-to-all-start.1 = ((bf16[128,5,3584]{2,1,0:T(8,128)(2,1)}), bf16[128,5,3584]{2,1,0:T(8,128)(2,1)}, u32[]{:S(2)}, u32[]{:S(2)}) async-start(bf16[128,5,3584]{2,1,0:T(8,128)(2,1)} %get-tuple-element.4), calls=%async_computation.1 | async-start | bytes 14680064 | tf_op jit(solution)/shard_map/all_to_all | solution.py:77
  278.4 97.7 %copy-start.5 = (f32[128,8]{0,1:T(8,128)S(1)}, f32[128,8]{0,1:T(8,128)}, u32[]{:S(2)}) copy-start(f32[128,8]{0,1:T(8,128)} %param.11) | copy-start | bytes 12292
  370.7 106.4 %all-to-all-start.2 = ((bf16[128,5,3584]{2,1,0:T(8,128)(2,1)}), bf16[128,5,3584]{2,1,0:T(8,128)(2,1)}, u32[]{:S(2)}, u32[]{:S(2)}) async-start(bf16[128,5,3584]{2,1,0:T(8,128)(2,1)} %copy.58), calls=%async_computation.2 | async-start | bytes 14680064 | tf_op jit(solution)/shard_map/all_to_all | solution.py:78
  503.0 10.1 %copy-start.1 = (bf16[128,3584]{1,0:T(8,128)(2,1)S(1)}, bf16[128,3584]{1,0:T(8,128)(2,1)}, u32[]{:S(2)}) copy-start(bf16[128,3584]{1,0:T(8,128)(2,1)} %param.8) | copy-start | bytes 2752516
where the time goes:
time: 522 us; the launch traced here: 514 us
  waiting for transfers between devices  167 us (32%)
  local copies, waits for them, and re-layouts  130 us (25%)
  blocking collectives  114 us (22%)
  matrix products  43.6 us (8%)
  other arithmetic  29.6 us (6%)
  starting transfers between devices  28.3 us (5%)
    all_to_all x1, blocking collectives, body(): lax.all_to_all(pair_send, ('edp', 'ep'), split_axis=0, concat_axis=0, til...  99 us
    all_to_all x1, waiting for transfers between devices, body(): lax.all_to_all(own_out, ('edp', 'ep'), split_axis=0, concat_axis=0, tiled...  92.3 us
    all_to_all x1, waiting for transfers between devices, body(): lax.all_to_all(partner_out, ('edp', 'ep'), split_axis=0, concat_axis=0, t...  74.3 us
    dot_general x1, matrix products, body(): jnp.dot(hidden, w_down[0], preferred_element_type=jnp.float32)  16.3 us
    all_to_all x1, blocking collectives, sent_and_summed(): lax.all_to_all(parts, axis, split_axis=0, concat_axis=0, tiled=True)  15.2 us
    reshape x1, local copies, waits for them, and re-layouts, body(): row_block = received.reshape(-1, model_width)  14.6 us
    reshape x1, local copies, waits for them, and re-layouts, body(): both_out = result.reshape(in_shape)  14.2 us
    dot_general x1, matrix products, body(): up_act = jnp.dot(row_block, w_up[0], preferred_element_type=jnp.float32)  13.7 us
  transfers between devices with their start and end apart: 5, of which 2 were waited for; matrix products, arithmetic and copies ran while one was open for 27% of the time, Pallas kernels for 0%

commit v1 on v0

v1 whole, which is shorter than its diff:
```python
import jax
import jax.numpy as jnp
from jax import lax
from jax.experimental import pallas as pl
from jax.experimental.pallas import tpu as pltpu
from jax.sharding import Mesh, PartitionSpec as P

PAIRS, HEAD, TAIL, WIDE = 64, 8, 2, 28
SLOTS = HEAD + TAIL
TAIL_AT, COEF_AT = HEAD * WIDE, SLOTS * WIDE
IN_ROWS = COEF_AT + 8
F32, BF16, I32 = jnp.float32, jnp.bfloat16, jnp.int32


def iota(shape, dim):
    return lax.broadcasted_iota(I32, shape, dim)


def pair_of(node_ref, local_ref, column):
    return node_ref[column : column + 1, :] * 8 + local_ref[2 * column : 2 * column + 1, :] // 2


def hits(node_ref, local_ref, pair):
    found = jnp.zeros(pair.shape, jnp.bool_)
    for column in range(4):
        found = found | (pair == pair_of(node_ref, local_ref, column))
    return found


def picks(node_ref, local_ref):
    tok = node_ref.shape[1]
    earlier = (iota((tok, tok), 0) < iota((tok, tok), 1)).astype(BF16)
    row = iota((PAIRS * HEAD, tok), 0)
    head_hit = hits(node_ref, local_ref, row // HEAD)
    head_rank = jnp.dot(head_hit.astype(F32).astype(BF16), earlier, preferred_element_type=F32)
    head = jnp.where(head_hit & (head_rank == (row % HEAD).astype(F32)), 1.0, 0.0)
    hit = hits(node_ref, local_ref, iota((PAIRS, tok), 0))
    rank = jnp.dot(hit.astype(F32).astype(BF16), earlier, preferred_element_type=F32)
    each = [jnp.where(hit & (rank == float(slot)), 1.0, 0.0) for slot in range(SLOTS)]
    return head, each


def send_kernel(node_ref, local_ref, aff_ref, tok_ref, out_ref, tail_ref):
    head, each = picks(node_ref, local_ref)
    head = head.astype(BF16)
    tail = jnp.concatenate(each[HEAD:], axis=0).astype(BF16)
    for k in range(7):
        rows = jnp.dot(head, tok_ref[:, 512 * k : 512 * (k + 1)], preferred_element_type=F32)
        for m in range(4):
            j = 4 * k + m
            tile = rows[:, 128 * m : 128 * (m + 1)].reshape(PAIRS, HEAD, 128)
            out_ref[:, 8 * j : 8 * j + 8, :] = tile.astype(BF16)
        rows = jnp.dot(tail, tok_ref[:, 512 * k : 512 * (k + 1)], preferred_element_type=F32)
        for m in range(4):
            for s in range(TAIL):
                tail_ref[pl.ds(s * WIDE + 4 * k + m, PAIRS, stride=TAIL * WIDE), :] = rows[
                    PAIRS * s : PAIRS * (s + 1), 128 * m : 128 * (m + 1)
                ]
    out_ref[:, TAIL_AT:COEF_AT, :] = tail_ref[...].reshape(PAIRS, TAIL * WIDE, 128).astype(BF16)
    aff = aff_ref[...]
    weight = 2.5 * aff / jnp.sum(aff, axis=0, keepdims=True)
    tok = node_ref.shape[1]
    pair = iota((PAIRS, tok), 0)
    even = jnp.zeros((PAIRS, tok), F32)
    odd = jnp.zeros((PAIRS, tok), F32)
    for column in range(4):
        first, second = weight[2 * column : 2 * column + 1, :], weight[2 * column + 1 : 2 * column + 2, :]
        flip = local_ref[2 * column : 2 * column + 1, :] % 2 == 1
        here = pair == pair_of(node_ref, local_ref, column)
        even = jnp.where(here, jnp.where(flip, second, first), even)
        odd = jnp.where(here, jnp.where(flip, first, second), odd)
    lane = iota((PAIRS, 128), 1)
    coef = jnp.zeros((PAIRS, 128), F32)
    for slot in range(SLOTS):
        even_w = jnp.sum(each[slot] * even, axis=1, keepdims=True)
        odd_w = jnp.sum(each[slot] * odd, axis=1, keepdims=True)
        coef = jnp.where(lane // 2 == 2 * slot, even_w, coef)
        coef = jnp.where(lane // 2 == 2 * slot + 1, odd_w, coef)
    high = coef.astype(BF16).astype(F32)
    coef = jnp.where(lane % 2 == 0, high, coef - high)
    out_ref[:, COEF_AT:IN_ROWS, :] = jnp.broadcast_to(coef[:, None, :], (PAIRS, 8, 128)).astype(BF16)


def unpack(in_ref, rows_ref, tail_ref):
    for j in range(WIDE):
        tile = in_ref[:, 8 * j : 8 * j + 8, :].astype(F32).reshape(PAIRS * HEAD, 128)
        rows_ref[: PAIRS * HEAD, 128 * j : 128 * (j + 1)] = tile.astype(BF16)
    tail_ref[...] = in_ref[:, TAIL_AT:COEF_AT, :].astype(F32).reshape(PAIRS * TAIL * WIDE, 128)
    for s in range(TAIL):
        at = PAIRS * (HEAD + s)
        for j in range(WIDE):
            tile = tail_ref[pl.ds(s * WIDE + j, PAIRS, stride=TAIL * WIDE), :]
            rows_ref[at : at + PAIRS, 128 * j : 128 * (j + 1)] = tile.astype(BF16)


def expert_kernel(core_ref, in_ref, gate_ref, up_ref, down_ref, out_ref, rows_ref, hid_ref, w_ref, tail_ref):
    step = pl.program_id(0)

    @pl.when(step == 0)
    def _():
        unpack(in_ref, rows_ref, tail_ref)
        core = core_ref[0]
        coef = in_ref[:, COEF_AT:IN_ROWS, :].astype(F32).reshape(PAIRS * 8, 128)
        tail_ref[: PAIRS * 8, :] = coef
        row, lane = iota((PAIRS * 8, 128), 0), iota((PAIRS * 8, 128), 1)
        mine = jnp.where(lane // 2 == 2 * (row % 8) + core, coef, 0.0)
        w_ref[: PAIRS * HEAD, :] = jnp.broadcast_to(jnp.sum(mine, axis=1, keepdims=True), (PAIRS * 8, 128))
        coef = tail_ref[pl.ds(0, PAIRS, stride=8), :]
        lane = iota((PAIRS, 128), 1)
        for s in range(TAIL):
            mine = jnp.where(lane // 2 == 2 * (HEAD + s) + core, coef, 0.0)
            at = PAIRS * (HEAD + s)
            w_ref[at : at + PAIRS, :] = jnp.broadcast_to(jnp.sum(mine, axis=1, keepdims=True), (PAIRS, 128))

    @pl.when(step < 4)
    def _():
        rows = rows_ref[...]
        gate = jnp.dot(rows, gate_ref[0], preferred_element_type=F32)
        up = jnp.dot(rows, up_ref[0], preferred_element_type=F32)
        hidden = gate / (1.0 + jnp.exp(-gate)) * up
        hid_ref[:, pl.ds(pl.multiple_of(step * 256, 256), 256)] = hidden.astype(BF16)

    @pl.when(step >= 4)
    def _():
        block = step - 4
        value = jnp.dot(hid_ref[...], down_ref[0], preferred_element_type=F32)
        w = w_ref[...]
        for m in range(4):
            part = value[:, 128 * m : 128 * (m + 1)] * w
            tile = part[: PAIRS * HEAD].reshape(PAIRS, HEAD, 128).astype(BF16)
            out_ref[:, pl.ds(pl.multiple_of(32 * block + 8 * m, 8), 8), :] = tile
            for s in range(TAIL):
                at = PAIRS * (HEAD + s)
                tail_ref[pl.ds(s * WIDE + 4 * block + m, PAIRS, stride=TAIL * WIDE), :] = part[at : at + PAIRS]

    @pl.when(step == 10)
    def _():
        out_ref[:, TAIL_AT:COEF_AT, :] = tail_ref[...].reshape(PAIRS, TAIL * WIDE, 128).astype(BF16)


def mix_kernel(node_ref, local_ref, in_ref, out_ref, rows_ref, tail_ref):
    head, each = picks(node_ref, local_ref)
    pick = jnp.concatenate([head] + each[HEAD:], axis=0).astype(BF16)
    unpack(in_ref, rows_ref, tail_ref)
    for k in range(7):
        at = slice(512 * k, 512 * (k + 1))
        value = lax.dot_general(pick, rows_ref[:, at], (((0,), (0,)), ((), ())), preferred_element_type=F32)
        out_ref[:, at] = value.astype(BF16)


def vmem(mib):
    return pltpu.CompilerParams(vmem_limit_bytes=mib << 20)


def body(tokens, node_ids, local_ids, affinity, w_gate, w_up, w_down, grad_parts):
    tok, width = tokens.shape
    nodes, locals_ = node_ids.T, local_ids.T
    tail = pltpu.VMEM((PAIRS * TAIL * WIDE, 128), F32)
    rows = pltpu.VMEM((PAIRS * SLOTS, width), BF16)
    chips = ("edp", "chip")
    message = pl.pallas_call(
        send_kernel,
        out_shape=jax.ShapeDtypeStruct((PAIRS, IN_ROWS, 128), BF16),
        scratch_shapes=[tail],
        compiler_params=vmem(32),
        name="send",
    )(nodes, locals_, affinity.T, tokens)
    own = lax.all_to_all(message, chips, split_axis=0, concat_axis=0, tiled=True)
    swap = [(0, 1), (1, 0)]
    other = lax.ppermute(own, "core", swap)
    core = lax.axis_index("core").astype(I32).reshape(1)
    experts = pl.pallas_call(
        expert_kernel,
        grid=(11,),
        in_specs=[
            pl.BlockSpec(memory_space=pltpu.SMEM),
            pl.BlockSpec((PAIRS, IN_ROWS, 128), lambda i: (0, 0, 0)),
            pl.BlockSpec((1, width, 256), lambda i: (0, 0, jnp.minimum(i, 3))),
            pl.BlockSpec((1, width, 256), lambda i: (0, 0, jnp.minimum(i, 3))),
            pl.BlockSpec((1, 1024, 512), lambda i: (0, 0, jnp.maximum(i - 4, 0))),
        ],
        out_specs=pl.BlockSpec((PAIRS, COEF_AT, 128), lambda i: (0, 0, 0)),
        out_shape=jax.ShapeDtypeStruct((PAIRS, COEF_AT, 128), BF16),
        scratch_shapes=[
            rows,
            pltpu.VMEM((PAIRS * SLOTS, 1024), BF16),
            pltpu.VMEM((PAIRS * SLOTS, 128), F32),
            tail,
        ],
        compiler_params=vmem(56),
        name="experts",
    )
    for_other = experts(core, other, w_gate, w_up, w_down)
    back = lax.ppermute(for_other, "core", swap)
    mine = experts(core, own, w_gate, w_up, w_down)
    both = (mine.astype(F32) + back.astype(F32)).astype(BF16)
    returned = lax.all_to_all(both, chips, split_axis=0, concat_axis=0, tiled=True)
    mixed = pl.pallas_call(
        mix_kernel,
        out_shape=jax.ShapeDtypeStruct((tok, width), BF16),
        scratch_shapes=[rows, tail],
        compiler_params=vmem(32),
        name="mix",
    )(nodes, locals_, returned)
    halves = grad_parts[0].reshape(PAIRS, 2, WIDE, 128)
    first, second = halves[:, 0], halves[:, 1]
    keep = jnp.where(core[0] == 0, first, second)
    give = jnp.where(core[0] == 0, second, first).astype(BF16)
    got = lax.ppermute(give, "core", swap)
    pair_sum = (keep + got.astype(F32)).astype(BF16)
    parts = lax.all_to_all(pair_sum, chips, split_axis=0, concat_axis=0, tiled=True)
    router_grad = parts.astype(F32).sum(axis=0)
    return mixed, router_grad


def solution(mesh):
    split = Mesh(mesh.devices.reshape(2, 32, 2), ("edp", "chip", "core"))
    every = ("edp", "chip", "core")
    flat, deep = P(every, None), P(every, None, None)
    return jax.shard_map(
        body,
        mesh=split,
        in_specs=(flat, flat, flat, flat, deep, deep, deep, deep),
        out_specs=(flat, flat),
        check_vma=False,
    )
```

time: 522 us -> 237 us (0.45)
  local copies, waits for them, and re-layouts: 130 us -> 4.76 us
  waiting for transfers between devices: 167 us -> 71.5 us
  Pallas kernels: 0 us -> 58.5 us
  blocking collectives: 114 us -> 67.9 us
  matrix products: 43.6 us -> 0 us
  other arithmetic: 29.6 us -> 8.88 us
  starting transfers between devices: 28.3 us -> 20.4 us
    all_to_all x3 -> x2, waiting for transfers between devices: 167 us -> 56.8 us  [the longest x1 56.8 us: body(): lax.all_to_all(both, chips, split_axis=0, concat_axis=0, tiled=True)]
    reshape x7 -> x0, local copies, waits for them, and re-layouts: 60 us -> none  [the longest x1 14.6 us: body(): row_block = received.reshape(-1, model_width)]
    pallas_call x0 -> x4, Pallas kernels: none -> 58.5 us  [the longest x1 25.8 us: body(): for_other = experts(core, other, w_gate, w_up, w_down)]
    all_to_all x2 -> x1, blocking collectives: 114 us -> 67.9 us  [body(): lax.all_to_all(message, chips, split_axis=0, concat_axis=0, tiled=True)]
    dot_general x3 -> x0, matrix products: 43.6 us -> none  [the longest x1 16.3 us: body(): jnp.dot(hidden, w_down[0], preferred_element_type=jnp.float32)]
    gather x4 -> x0, local copies, waits for them, and re-layouts: 34.6 us -> none  [the longest x2 13 us: body(): pair_picked = tokens[jnp.maximum(pair_owner - 1, 0) // node_pick]]
    ppermute x2 -> x3, waiting for transfers between devices: 0.01 us -> 14.7 us  [the longest x1 8.25 us: body(): other = lax.ppermute(own, 'core', swap)]
    slice x4 -> x0, local copies, waits for them, and re-layouts: 14.4 us -> none  [the longest x1 10.5 us: body(): own_out = both_out[:, :half_cap]]
  transfers between devices with their start and end apart: 5 -> 5, of which waited for: 2 -> 3; matrix products, arithmetic and copies ran while one was open for 27% -> 4% of each run, Pallas kernels for 0% -> 11%
where the time goes in v1:
time: 237 us; the launch traced here: 233 us
  waiting for transfers between devices  71.5 us (30%)
  blocking collectives  67.9 us (29%)
  Pallas kernels  58.5 us (25%)
  starting transfers between devices  20.4 us (9%)
  other arithmetic  8.88 us (4%)
  local copies, waits for them, and re-layouts  4.76 us (2%)
    all_to_all x1, blocking collectives, body(): lax.all_to_all(message, chips, split_axis=0, concat_axis=0, tiled=True)  67.9 us
    all_to_all x1, waiting for transfers between devices, body(): lax.all_to_all(both, chips, split_axis=0, concat_axis=0, tiled=True)  56.8 us
    pallas_call x1, Pallas kernels, body(): for_other = experts(core, other, w_gate, w_up, w_down)  25.8 us
    pallas_call x1, Pallas kernels, body(): mine = experts(core, own, w_gate, w_up, w_down)  25.7 us
    all_to_all x1, starting transfers between devices, body(): lax.all_to_all(both, chips, split_axis=0, concat_axis=0, tiled=True)  10.5 us
    all_to_all x1, starting transfers between devices, body(): lax.all_to_all(pair_sum, chips, split_axis=0, concat_axis=0, tiled=True)  9.25 us
    ppermute x1, waiting for transfers between devices, body(): other = lax.ppermute(own, 'core', swap)  8.25 us
    convert_element_type x1, other arithmetic, body(): both = (mine.astype(F32) + back.astype(F32)).astype(BF16)  6.96 us
  transfers between devices with their start and end apart: 5, of which 3 were waited for; matrix products, arithmetic and copies ran while one was open for 4% of the time, Pallas kernels for 11%

profile of v1, /device:TPU:10, one launch (start us, length us, event | category | flops | bytes accessed | tf_op | source)
XLA Modules:
  0.0 232.6 jit_solution(12935303746028093300)
XLA Ops:
  0.6 0.0 copy-start
  0.6 1.2 copy-done
  1.8 0.0 copy-start.1
  1.8 0.7 copy-done.1
  2.5 0.0 copy-start.3
  2.5 0.7 copy-done.3
  3.2 0.0 copy-start.5
  3.2 0.7 copy-done.5
  3.9 1.6 send.1
  5.5 67.9 %all_to_all.15.in_ref = bf16[64,288,128]{2,1,0:T(8,128)(2,1)} all-to-all(bf16[64,288,128]{2,1,0:T(8,128)(2,1)S(1)} %send.1), channel_id=1, replica_groups=mesh['edp'=2,'chip'=32,'core'=2] {'edp','chip'}, dimensions={0} | all-to-all | bytes 9437184 | tf_op jit(solution)/shard_map/all_to_all | solution.py:168
  73.4 0.0 collective-permute-start
  73.4 8.2 %collective-permute-done.in_ref = bf16[64,288,128]{2,1,0:T(8,128)(2,1)} collective-permute-done((bf16[64,288,128]{2,1,0:T(8,128)(2,1)}, bf16[64,288,128]{2,1,0:T(8,128)(2,1)}, u32[]{:S(2)}, u32[]{:S(2)}) %collective-permute-start) | collective-permute-done | bytes 4718624 | tf_op jit(solution)/shard_map/ppermute | solution.py:170
  81.6 25.8 %experts.3 = bf16[64,280,128]{2,1,0:T(8,128)(2,1)} custom-call(s32[1]{0:T(128)} %bitcast.2.core_ref, bf16[64,288,128]{2,1,0:T(8,128)(2,1)} %collective-permute-done.in_ref, bf16[1,3584,1024]{2,1,0:T(8,128)(2,1)} %gate_ref.3, bf16[1,3584,1024]{2,1,0:T(8,128)(2,1)} %up_ref.3, bf16[1,1024,3584]{2,1,0:T(8,128)(2,1)} %down_ref.3), custom_call_target="tpu_custom_call" | custom-call | tf_op jit(solution)/shard_map/experts/pallas_call | solution.py:193
  107.4 0.1 collective-permute-start.1
  107.5 1.5 reshape_squeeze.3
  109.1 0.1 fusion.3
  109.2 0.5 collective-permute-start.2
  109.6 6.5 %collective-permute-done.2 = bf16[64,28,128]{2,1,0:T(8,128)(2,1)S(1)} collective-permute-done((bf16[64,28,128]{2,1,0:T(8,128)(2,1)S(1)}, bf16[64,28,128]{2,1,0:T(8,128)(2,1)S(1)}, u32[]{:S(2)}, u32[]{:S(2)}) %collective-permute-start.2) | collective-permute-done | bytes 458784 | tf_op jit(solution)/shard_map/ppermute | solution.py:209
  116.1 1.1 fusion.2
  117.2 9.2 %all-to-all-start.2 = ((bf16[64,28,128]{2,1,0:T(8,128)(2,1)}), bf16[64,28,128]{2,1,0:T(8,128)(2,1)S(1)}, u32[]{:S(2)}, u32[]{:S(2)}) async-start(bf16[64,28,128]{2,1,0:T(8,128)(2,1)} %fusion.2), calls=%async_computation.2 | async-start | bytes 1048576 | tf_op jit(solution)/shard_map/all_to_all | solution.py:211
  126.4 25.7 %experts.2 = bf16[64,280,128]{2,1,0:T(8,128)(2,1)} custom-call(s32[1]{0:T(128)} %bitcast.2.core_ref, bf16[64,288,128]{2,1,0:T(8,128)(2,1)} %all_to_all.15.in_ref, bf16[1,3584,1024]{2,1,0:T(8,128)(2,1)} %gate_ref.3, bf16[1,3584,1024]{2,1,0:T(8,128)(2,1)} %up_ref.3, bf16[1,1024,3584]{2,1,0:T(8,128)(2,1)} %down_ref.3), custom_call_target="tpu_custom_call" | custom-call | tf_op jit(solution)/shard_map/experts/pallas_call | solution.py:195
  152.1 0.0 collective-permute-done.1
  152.1 7.0 %add_convert_fusion = bf16[64,280,128]{2,1,0:T(8,128)(2,1)} fusion(bf16[64,280,128]{2,1,0:T(8,128)(2,1)} %collective-permute-done.1, bf16[64,280,128]{2,1,0:T(8,128)(2,1)} %experts.2), kind=kLoop, calls=%fused_computation | loop fusion | flops 9175040 | bytes 13762560 | tf_op jit(solution)/shard_map/convert_element_type | solution.py:196
  159.1 0.0 copy-start.2
  159.1 0.0 copy-start.4
  159.1 0.0 all-to-all-done.2
  159.1 10.5 %all-to-all-start.1 = ((bf16[64,280,128]{2,1,0:T(8,128)(2,1)}), bf16[64,280,128]{2,1,0:T(8,128)(2,1)}, u32[]{:S(2)}, u32[]{:S(2)}) async-start(bf16[64,280,128]{2,1,0:T(8,128)(2,1)} %add_convert_fusion), calls=%async_computation.1 | async-start | bytes 9175040 | tf_op jit(solution)/shard_map/all_to_all | solution.py:197
  169.6 0.7 convert_reduce_fusion
  170.4 56.8 %all-to-all-done.1.in_ref = bf16[64,280,128]{2,1,0:T(8,128)(2,1)} async-done(((bf16[64,280,128]{2,1,0:T(8,128)(2,1)}), bf16[64,280,128]{2,1,0:T(8,128)(2,1)}, u32[]{:S(2)}, u32[]{:S(2)}) %all-to-all-start.1) | async-done | bytes 4587552 | tf_op jit(solution)/shard_map/all_to_all | solution.py:197
  227.2 0.0 copy-done.2
  227.2 0.0 copy-done.4
  227.2 5.4 %mix.1 = bf16[128,3584]{1,0:T(8,128)(2,1)} custom-call(s32[4,128]{1,0:T(4,128)S(1)} %bitcast.31, s32[8,128]{1,0:T(8,128)S(1)} %bitcast.29, bf16[64,280,128]{2,1,0:T(8,128)(2,1)} %all-to-all-done.1.in_ref), custom_call_target="tpu_custom_call" | custom-call | tf_op jit(solution)/shard_map/mix/pallas_call | solution.py:198
Async XLA Ops:
  0.6 1.2 copy-start
  1.8 0.7 copy-start.1
  2.5 0.7 copy-start.3
  3.2 0.7 copy-start.5
  73.4 8.3 %collective-permute-start = (bf16[64,288,128]{2,1,0:T(8,128)(2,1)}, bf16[64,288,128]{2,1,0:T(8,128)(2,1)}, u32[]{:S(2)}, u32[]{:S(2)}) collective-permute-start(bf16[64,288,128]{2,1,0:T(8,128)(2,1)} %all_to_all.15.in_ref), channel_id=1, source_target_pairs={{0,1},{1,0},{2,3},{3,2},{4,5},{5,4},{6,7},{7,6},{8,9},{9,8},{10,11... | collective-permute-start | bytes 14155784 | tf_op jit(solution)/shard_map/ppermute | solution.py:170
  107.4 44.7 %collective-permute-start.1 = (bf16[64,280,128]{2,1,0:T(8,128)(2,1)}, bf16[64,280,128]{2,1,0:T(8,128)(2,1)}, u32[]{:S(2)}, u32[]{:S(2)}) collective-permute-start(bf16[64,280,128]{2,1,0:T(8,128)(2,1)} %experts.3), channel_id=1, source_target_pairs={{0,1},{1,0},{2,3},{3,2},{4,5},{5,4},{6,7},{7,6},{8,9},{9,8},{10,11... | collective-permute-start | bytes 13762568 | tf_op jit(solution)/shard_map/ppermute | solution.py:194
  109.2 6.9 %collective-permute-start.2 = (bf16[64,28,128]{2,1,0:T(8,128)(2,1)S(1)}, bf16[64,28,128]{2,1,0:T(8,128)(2,1)S(1)}, u32[]{:S(2)}, u32[]{:S(2)}) collective-permute-start(bf16[64,28,128]{2,1,0:T(8,128)(2,1)S(1)} %fusion.3), channel_id=1, source_target_pairs={{0,1},{1,0},{2,3},{3,2},{4,5},{5,4},{6,7},{7,6},{8,9},{9,8},{10,11... | collective-permute-start | bytes 1376264 | tf_op jit(solution)/shard_map/ppermute | solution.py:209
  117.2 41.9 %all-to-all-start.2 = ((bf16[64,28,128]{2,1,0:T(8,128)(2,1)}), bf16[64,28,128]{2,1,0:T(8,128)(2,1)S(1)}, u32[]{:S(2)}, u32[]{:S(2)}) async-start(bf16[64,28,128]{2,1,0:T(8,128)(2,1)} %fusion.2), calls=%async_computation.2 | async-start | bytes 1048576 | tf_op jit(solution)/shard_map/all_to_all | solution.py:211
  159.1 68.1 %copy-start.2 = (s32[128,8]{0,1:T(8,128)S(1)}, s32[128,8]{0,1:T(8,128)}, u32[]{:S(2)}) copy-start(s32[128,8]{0,1:T(8,128)} %param.10) | copy-start | bytes 12292
  159.1 68.1 %copy-start.4 = (s32[128,4]{0,1:T(4,128)S(1)}, s32[128,4]{0,1:T(4,128)}, u32[]{:S(2)}) copy-start(s32[128,4]{0,1:T(4,128)} %param.9) | copy-start | bytes 6148
  159.1 68.1 %all-to-all-start.1 = ((bf16[64,280,128]{2,1,0:T(8,128)(2,1)}), bf16[64,280,128]{2,1,0:T(8,128)(2,1)}, u32[]{:S(2)}, u32[]{:S(2)}) async-start(bf16[64,280,128]{2,1,0:T(8,128)(2,1)} %add_convert_fusion), calls=%async_computation.1 | async-start | bytes 9175040 | tf_op jit(solution)/shard_map/all_to_all | solution.py:197
